TPU v7x, 32 devices: a whole 2x2x4 slice. The times are simulated.
32 devices in a mesh: section: 2 (over x), seq: 8 (over z, y), rep: 2 (over core).
Axes of the slice: x: 2, y: 2, z: 4, core: 2. Of those that a mesh axis runs over, the one named last changes fastest.
Arguments:
- queries: bfloat16 [512, 2560], P('seq', ('section', 'rep')), may hold values from -5 to 5
- keys: bfloat16 [512, 2560], P('seq', ('section', 'rep')), may hold values from -5 to 5
- values: bfloat16 [512, 2560], P('seq', ('section', 'rep')), may hold values from -6 to 6
- block_order: int32 [16], replicated, may hold values from 0 to 15, each once
- wo: bfloat16 [2560, 5120], P(('section', 'rep'), 'seq'), may hold values from -0.125 to 0.125
- resid: bfloat16 [4, 5120, 128], P(('section', 'rep'), 'seq'), may hold values from -60 to 60
- gain: bfloat16 [5120], P('seq'), may hold values from 0.099609375 to 1.8984375
- w_gate: bfloat16 [13824, 5120], P('seq'), may hold values from -0.078125 to 0.078125
- w_up: bfloat16 [13824, 5120], P('seq'), may hold values from -0.078125 to 0.078125
- w_down: bfloat16 [13824, 5120], P('seq'), may hold values from -0.0625 to 0.0625
Outputs:
- mixed: bfloat16 [4, 5120, 128], P(('section', 'rep'), 'seq')
Inputs may be any that keep to these rules, and one draw needn't show every extreme that they name: `block_order`: each number once.
All inputs are finite; a program needn't handle non-finite values.
Results may differ from a plain program's by a relative error of at most 0.0055.
Values may be sent and summed in bfloat16 or wider, within the bound.
A program may use at most 128 MiB of HBM per device.

v0:
```python
import jax
import jax.numpy as jnp
from jax import lax
from jax.sharding import PartitionSpec as P

D = 5120
HEAD_DIM = 128


def key_positions(order, start, count, block_rows):
    row_ids = start + jnp.arange(count, dtype=jnp.int32)
    owners = row_ids // block_rows
    match = owners[:, None] == jnp.arange(order.shape[0], dtype=jnp.int32)[None, :]
    first = jnp.sum(jnp.where(match, order[None, :], 0), axis=1)
    return first * block_rows + row_ids % block_rows


def on_device(queries, keys, values, block_order, wo, resid, gain, w_gate, w_up, w_down):
    seq_dev = queries.shape[0]
    heads_dev = queries.shape[1] // HEAD_DIM
    groups = lax.axis_size("section") * lax.axis_size("rep")
    n_seq = lax.axis_size("seq")
    sub_rows = seq_dev // groups
    block_rows = seq_dev // 2
    query_start = lax.axis_index("seq") * seq_dev
    query_pos = key_positions(block_order, query_start, seq_dev, block_rows)
    query_heads = queries.reshape(seq_dev, heads_dev, HEAD_DIM)
    scale = HEAD_DIM ** (-0.5)
    running_max = jnp.full((seq_dev, heads_dev), -1e30, jnp.float32)
    key_piece = lax.all_gather(keys, "seq", axis=0, tiled=True)
    value_piece = lax.all_gather(values, "seq", axis=0, tiled=True)
    count = key_piece.shape[0]
    key_pos = key_positions(block_order, jnp.int32(0), count, block_rows)
    scores = (
        jnp.einsum(
            "qhd,khd->qhk",
            query_heads,
            key_piece.reshape(count, heads_dev, HEAD_DIM),
            preferred_element_type=jnp.float32,
        )
        * scale
    )
    visible = (key_pos[None, :] <= query_pos[:, None])[:, None, :]
    new_max = jnp.maximum(running_max, jnp.max(jnp.where(visible, scores, -1e30), axis=-1))
    probs = jnp.where(visible, jnp.exp(scores - new_max[..., None]), 0.0)
    total = jnp.sum(probs, axis=-1)
    weighted = jnp.einsum(
        "qhk,khd->qhd",
        probs.astype(jnp.bfloat16),
        value_piece.reshape(count, heads_dev, HEAD_DIM),
        preferred_element_type=jnp.float32,
    )
    running_max, total, weighted = (new_max, total, weighted)
    attended = (
        (weighted / total[..., None]).astype(jnp.bfloat16).reshape(seq_dev, heads_dev * HEAD_DIM)
    )
    columns = wo.shape[1]
    token_count = n_seq * sub_rows
    parts = attended.reshape(groups, sub_rows, heads_dev * HEAD_DIM)
    group_rows = lax.all_to_all(parts, ("section", "rep"), split_axis=0, concat_axis=2, tiled=True)
    wo_columns = lax.all_gather(wo, ("section", "rep"), axis=0, tiled=True)
    piece = lax.all_gather(group_rows, "seq", axis=0, tiled=True)
    flat = piece.reshape(piece.shape[0] * piece.shape[1], piece.shape[2])
    product = jnp.dot(flat, wo_columns, preferred_element_type=jnp.float32)
    projected = product.reshape(piece.shape[0], piece.shape[1], columns)
    projected_cols = projected.reshape(token_count, columns).T
    carried = resid.reshape(columns, token_count).astype(jnp.float32) + projected_cols
    squares = lax.psum(jnp.sum(carried * carried, axis=0), "seq")
    normed = (
        carried * lax.rsqrt(squares / D + 1e-05)[None, :] * gain.astype(jnp.float32)[:, None]
    ).astype(jnp.bfloat16)
    piece = lax.all_gather(normed, "seq", axis=0, tiled=True)
    gate_sum = jnp.dot(w_gate, piece, preferred_element_type=jnp.float32)
    up_sum = jnp.dot(w_up, piece, preferred_element_type=jnp.float32)
    hidden = (jax.nn.silu(gate_sum) * up_sum).astype(jnp.bfloat16)
    term = lax.dot_general(
        w_down, hidden, (((0,), (0,)), ((), ())), preferred_element_type=jnp.float32
    )
    down = lax.psum_scatter(term, "seq", scatter_dimension=0, tiled=True)
    return (carried + down).astype(jnp.bfloat16).reshape(resid.shape)


def solution(mesh):
    return jax.shard_map(
        on_device,
        mesh=mesh,
        in_specs=(
            P("seq", ("section", "rep")),
            P("seq", ("section", "rep")),
            P("seq", ("section", "rep")),
            P(),
            P(("section", "rep"), "seq"),
            P(("section", "rep"), "seq", None),
            P("seq"),
            P("seq", None),
            P("seq", None),
            P("seq", None),
        ),
        out_specs=P(("section", "rep"), "seq", None),
        check_vma=False,
    )
```

profile of v0, /device:TPU:0, one launch (start us, length us, event | category | flops | bytes accessed | tf_op | source)
XLA Modules:
  0.0 288.4 jit_solution(9217807981591576571)
XLA Ops:
  6.5 0.7 all-gather.3.cloned.1.call-update
  7.3 33.6 %all_gather.15 = bf16[512,640]{1,0:T(8,128)(2,1)S(1)} all-gather(bf16[64,640]{1,0:T(8,128)(2,1)} %param.11), channel_id=1, replica_groups=mesh['section'=2,'seq'=8,'rep'=2] {'seq'}, dimensions={0}, use_global_device_ids=true | all-gather | bytes 737280 | tf_op jit(solution)/shard_map/all_gather | solution.py:30
  40.9 0.3 copy.33
  41.2 31.9 %all_gather.16 = bf16[512,640]{1,0:T(8,128)(2,1)S(1)} all-gather(bf16[64,640]{1,0:T(8,128)(2,1)} %param.12), channel_id=1, replica_groups=mesh['section'=2,'seq'=8,'rep'=2] {'seq'}, dimensions={0}, use_global_device_ids=true | all-gather | bytes 737280 | tf_op jit(solution)/shard_map/all_gather | solution.py:31
  73.1 0.3 copy.36
  73.4 0.1 select_reduce_fusion.2
  73.5 0.1 select_reduce_fusion.1
  73.7 0.3 select_reduce_fusion
  74.0 0.3 fusion.6
  74.3 0.4 fusion.5
  74.7 0.7 reshape_reshape.3
  75.5 3.3 %all-to-all-start = ((bf16[4,16,640]{2,1,0:T(8,128)(2,1)}), bf16[4,16,640]{2,1,0:T(8,128)(2,1)S(1)}, u32[]{:S(2)}, u32[]{:S(2)}) async-start(bf16[4,16,640]{2,1,0:T(8,128)(2,1)} %reshape_reshape.3), calls=%async_computation | async-start | bytes 163840 | tf_op jit(solution)/shard_map/all_to_all | solution.py:60
  78.9 0.2 copy.32
  79.0 3.9 %all-to-all-done = bf16[4,16,640]{2,1,0:T(8,128)(2,1)S(1)} async-done(((bf16[4,16,640]{2,1,0:T(8,128)(2,1)}), bf16[4,16,640]{2,1,0:T(8,128)(2,1)S(1)}, u32[]{:S(2)}, u32[]{:S(2)}) %all-to-all-start) | async-done | bytes 81952 | tf_op jit(solution)/shard_map/all_to_all | solution.py:60
  83.0 31.7 %all_gather.17 = bf16[8,16,2560]{2,1,0:T(8,128)(2,1)S(1)} all-gather(bf16[1,16,2560]{2,1,0:T(8,128)(2,1)S(1)} %bitcast.59), channel_id=1, replica_groups=mesh['section'=2,'seq'=8,'rep'=2] {'seq'}, dimensions={0}, use_global_device_ids=true | all-gather | bytes 737280 | tf_op jit(solution)/shard_map/all_gather | solution.py:62
  114.6 2.7 multiply_reduce_fusion
  117.3 21.5 %psum.7 = f32[128]{0:T(128)S(1)} all-reduce(f32[128]{0:T(128)S(1)} %get-tuple-element.7), channel_id=1, replica_groups=mesh['section'=2,'seq'=8,'rep'=2] {'seq'}, use_global_device_ids=true, to_apply=%region_5.6 | all-reduce | flops 128 | bytes 1024 | tf_op jit(solution)/shard_map/psum | solution.py:68
  138.9 0.8 multiply_convert_fusion
  139.7 38.9 %all-gather.5.cloned.1.call-done = bf16[5120,128]{0,1:T(8,128)(2,1)} async-done(((bf16[640,128]{0,1:T(8,128)(2,1)}), bf16[5120,128]{0,1:T(8,128)(2,1)}) %all-gather.5.cloned.1.call-update) | async-done | bytes 1310736 | tf_op jit(solution)/shard_map/all_gather | solution.py:72
  178.6 11.1 %convolution_bitcast_fusion.2 = f32[1728,128]{1,0:T(8,128)S(1)} fusion(bf16[5120,128]{0,1:T(8,128)(2,1)} %all-gather.5.cloned.1.call-done, bf16[1728,5120]{1,0:T(8,128)(2,1)} %param.17), kind=kOutput, calls=%fused_computation.3 | convolution fusion | flops 2264924160 | bytes 19890176 | tf_op jit(solution)/shard_map/dot_general | solution.py:73
  189.7 20.6 %convolution_bitcast_fusion = f32[5120,128]{0,1:T(8,128)} fusion(bf16[1728,5120]{1,0:T(8,128)(2,1)} %param.19, bf16[5120,128]{0,1:T(8,128)(2,1)S(1)} %copy-done.2, bf16[1728,5120]{1,0:T(8,128)(2,1)} %param.18, f32[1728,128]{1,0:T(8,128)S(1)} %convolution_bitcast_fusion.2), kind=kOutput, calls=%fused_computation | convolution fusion | flops 4531175424 | bytes 40206336 | tf_op jit(solution)/shard_map/dot_general | solution.py:76
  210.4 69.7 %reduce-scatter.2.cloned.1.call-done = f32[640,128]{0,1:T(8,128)} async-done(((f32[5120,128]{0,1:T(8,128)}), f32[640,128]{0,1:T(8,128)}) %reduce-scatter.2.cloned.1.call-update) | async-done | bytes 327696 | tf_op jit(solution)/shard_map/reduce_scatter | solution.py:79
  280.1 1.0 fusion.13
  281.1 0.8 copy.40
  (28 shorter events, 0.4 us)
Async XLA Ops:
  6.5 67.1 %copy-start = (bf16[64,640]{1,0:T(8,128)(2,1)S(1)}, bf16[64,640]{1,0:T(8,128)(2,1)}, u32[]{:S(2)}) copy-start(bf16[64,640]{1,0:T(8,128)(2,1)} %param.10) | copy-start | bytes 245764
  6.5 66.8 %copy-start.5 = (s32[16]{0:T(128)S(1)}, s32[16]{0:T(128)}, u32[]{:S(2)}) copy-start(s32[16]{0:T(128)} %param.13) | copy-start | bytes 196
  6.5 108.1 %all-gather.3.cloned.1.call-start = ((), (), s32[]{:S(2)}) async-start(), calls=%async_computation.2 | async-start | bytes 4096000 | tf_op jit(solution)/shard_map/all_gather | solution.py:61
  41.1 37.7 %copy-start.3 = (bf16[1,640,128]{2,1,0:T(8,128)(2,1)S(1)}, bf16[1,640,128]{2,1,0:T(8,128)(2,1)}, u32[]{:S(2)}) copy-start(bf16[1,640,128]{2,1,0:T(8,128)(2,1)} %param.15) | copy-start | bytes 491524
  73.1 5.9 %copy-start.4 = (bf16[640]{0:T(1024)(128)(2,1)S(1)}, bf16[640]{0:T(1024)(128)(2,1)}, u32[]{:S(2)}) copy-start(bf16[640]{0:T(1024)(128)(2,1)} %param.16) | copy-start | bytes 3844
  75.5 7.5 %all-to-all-start = ((bf16[4,16,640]{2,1,0:T(8,128)(2,1)}), bf16[4,16,640]{2,1,0:T(8,128)(2,1)S(1)}, u32[]{:S(2)}, u32[]{:S(2)}) async-start(bf16[4,16,640]{2,1,0:T(8,128)(2,1)} %reshape_reshape.3), calls=%async_computation | async-start | bytes 163840 | tf_op jit(solution)/shard_map/all_to_all | solution.py:60
  78.8 99.8 %all-gather.5.cloned.1.call-start = ((), (), s32[]{:S(2)}) async-start(), calls=%async_computation.3 | async-start | bytes 1474560 | tf_op jit(solution)/shard_map/all_gather | solution.py:72
  139.7 140.4 %reduce-scatter.2.cloned.1.call-start = ((), (), s32[]{:S(2)}) async-start(), calls=%async_computation.4 | async-start | bytes 2949120 | tf_op jit(solution)/shard_map/reduce_scatter | solution.py:79
  178.6 11.1 %copy-start.2 = (bf16[5120,128]{0,1:T(8,128)(2,1)S(1)}, bf16[5120,128]{0,1:T(8,128)(2,1)}, u32[]{:S(2)}) copy-start(bf16[5120,128]{0,1:T(8,128)(2,1)} %all-gather.5.cloned.1.call-done) | copy-start | bytes 3932164
  189.7 92.2 %copy-start.1 = (bf16[64,640]{1,0:T(8,128)(2,1)S(1)}, bf16[64,640]{1,0:T(8,128)(2,1)}, u32[]{:S(2)}) copy-start(bf16[64,640]{1,0:T(8,128)(2,1)} %param.10) | copy-start | bytes 245764
Sparse Core Ops, SparseCore 0:
  8.9 31.9 all-gather.2
  139.8 38.8 all-gather.4
  210.5 69.5 reduce-scatter.1
where the time goes:
time: 289 us; the launch traced here: 288 us
  blocking collectives  119 us (41%)
  waiting for transfers between devices  113 us (39%)
  matrix products  35.1 us (12%)
  between operations  13.3 us (5%)
  starting transfers between devices  3.38 us (1%)
    reduce_scatter x1, waiting for transfers between devices, on_device(): down = lax.psum_scatter(term, 'seq', scatter_dimension=0, tiled=True)  69.7 us
    all_gather x1, waiting for transfers between devices, on_device(): piece = lax.all_gather(normed, 'seq', axis=0, tiled=True)  38.9 us
    all_gather x1, blocking collectives, on_device(): key_piece = lax.all_gather(keys, 'seq', axis=0, tiled=True)  33.6 us
    all_gather x1, blocking collectives, on_device(): value_piece = lax.all_gather(values, 'seq', axis=0, tiled=True)  31.9 us
    all_gather x1, blocking collectives, on_device(): piece = lax.all_gather(group_rows, 'seq', axis=0, tiled=True)  31.7 us
    psum x1, blocking collectives, on_device(): squares = lax.psum(jnp.sum(carried * carried, axis=0), 'seq')  21.5 us
    dot_general x1, matrix products, on_device(): lax.dot_general(w_down, hidden, (((0,), (0,)), ((), ())), preferred_eleme...  20.6 us
    dot_general x1, matrix products, on_device(): gate_sum = jnp.dot(w_gate, piece, preferred_element_type=jnp.float32)  11.1 us
  transfers between devices with their start and end apart: 4, of which 3 were waited for; matrix products, arithmetic and copies ran while one was open for 1% of the time, Pallas kernels for 0%

commit v1 on v0

--- a/solution.py
+++ b/solution.py
@@ -27,7 +27,10 @@
     query_heads = queries.reshape(seq_dev, heads_dev, HEAD_DIM)
     scale = HEAD_DIM ** (-0.5)
     running_max = jnp.full((seq_dev, heads_dev), -1e30, jnp.float32)
-    key_piece = lax.all_gather(keys, "seq", axis=0, tiled=True)
+    size = lax.axis_size("seq")
+    blocks = jnp.stack([keys for _ in range(size)])
+    blocks = lax.all_to_all(blocks, "seq", split_axis=0, concat_axis=0)
+    key_piece = jnp.concatenate(blocks, axis=0)
     value_piece = lax.all_gather(values, "seq", axis=0, tiled=True)
     count = key_piece.shape[0]
     key_pos = key_positions(block_order, jnp.int32(0), count, block_rows)

time: 289 us -> 271 us (0.938)
  blocking collectives: 119 us -> 90.7 us
  starting transfers between devices: 3.38 us -> 10.7 us
    all_gather x1 -> x0, blocking collectives: 33.6 us -> none  [on_device(): key_piece = lax.all_gather(keys, 'seq', axis=0, tiled=True)]
    all_gather x1, blocking collectives: 31.9 us -> 41 us  [on_device(): value_piece = lax.all_gather(values, 'seq', axis=0, tiled=True)]
    all_to_all x0 -> x1, starting transfers between devices: none -> 7.31 us  [on_device(): blocks = lax.all_to_all(blocks, 'seq', split_axis=0, concat_axis=0)]
    psum x1, blocking collectives: 21.5 us -> 17.8 us  [on_device(): squares = lax.psum(jnp.sum(carried * carried, axis=0), 'seq')]
  transfers between devices with their start and end apart: 4 -> 5, of which waited for: 3 -> 3; matrix products, arithmetic and copies ran while one was open for 1% -> 2% of each run, Pallas kernels for 0% -> 0%
where the time goes in v1:
time: 271 us
  waiting for transfers between devices  114 us (42%)
  blocking collectives  90.7 us (33%)
  matrix products  35.2 us (13%)
  between operations  13.3 us (5%)
  starting transfers between devices  10.7 us (4%)
  local copies, waits for them, and re-layouts  4.58 us (2%)
    reduce_scatter x1, waiting for transfers between devices, on_device(): down = lax.psum_scatter(term, 'seq', scatter_dimension=0, tiled=True)  69.5 us
    all_gather x1, blocking collectives, on_device(): value_piece = lax.all_gather(values, 'seq', axis=0, tiled=True)  41 us
    all_gather x1, waiting for transfers between devices, on_device(): piece = lax.all_gather(normed, 'seq', axis=0, tiled=True)  39.7 us
    all_gather x1, blocking collectives, on_device(): piece = lax.all_gather(group_rows, 'seq', axis=0, tiled=True)  31.8 us
    dot_general x1, matrix products, on_device(): lax.dot_general(w_down, hidden, (((0,), (0,)), ((), ())), preferred_eleme...  20.6 us
    psum x1, blocking collectives, on_device(): squares = lax.psum(jnp.sum(carried * carried, axis=0), 'seq')  17.8 us
    dot_general x1, matrix products, on_device(): gate_sum = jnp.dot(w_gate, piece, preferred_element_type=jnp.float32)  11.1 us
    all_to_all x1, starting transfers between devices, on_device(): blocks = lax.all_to_all(blocks, 'seq', split_axis=0, concat_axis=0)  7.31 us
  transfers between devices with their start and end apart: 5, of which 3 were waited for; matrix products, arithmetic and copies ran while one was open for 2% of the time, Pallas kernels for 0%

profile of v1, /device:TPU:0, one launch (start us, length us, event | category | flops | bytes accessed | tf_op | source)
XLA Modules:
  0.0 270.8 jit_solution(10974706839600329962)
XLA Ops:
  6.5 0.7 all-gather.3.cloned.1.call-update
  7.3 1.8 stack.2
  9.0 7.3 %all-to-all-start = ((bf16[8,64,640]{2,1,0:T(8,128)(2,1)}), bf16[8,64,640]{2,1,0:T(8,128)(2,1)S(1)}, u32[]{:S(2)}, u32[]{:S(2)}) async-start(bf16[8,64,640]{2,1,0:T(8,128)(2,1)} %stack.2), calls=%async_computation | async-start | bytes 1310720 | tf_op jit(solution)/shard_map/all_to_all | solution.py:32
  16.3 41.0 %all_gather.12 = bf16[512,640]{1,0:T(8,128)(2,1)S(1)} all-gather(bf16[64,640]{1,0:T(8,128)(2,1)} %param.12), channel_id=1, replica_groups=mesh['section'=2,'seq'=8,'rep'=2] {'seq'}, dimensions={0}, use_global_device_ids=true | all-gather | bytes 737280 | tf_op jit(solution)/shard_map/all_gather | solution.py:34
  57.4 0.3 copy.33
  57.7 0.1 select_reduce_fusion.2
  58.0 0.7 reshape_reshape.6
  58.8 0.4 select_reduce_fusion
  59.2 0.3 fusion.7
  59.5 0.4 fusion.5
  60.0 0.7 reshape_reshape.7
  60.7 3.3 %all-to-all-start.1 = ((bf16[4,16,640]{2,1,0:T(8,128)(2,1)}), bf16[4,16,640]{2,1,0:T(8,128)(2,1)S(1)}, u32[]{:S(2)}, u32[]{:S(2)}) async-start(bf16[4,16,640]{2,1,0:T(8,128)(2,1)} %reshape_reshape.7), calls=%async_computation.1 | async-start | bytes 163840 | tf_op jit(solution)/shard_map/all_to_all | solution.py:63
  64.1 0.2 copy.30
  64.3 3.9 %all-to-all-done.1 = bf16[4,16,640]{2,1,0:T(8,128)(2,1)S(1)} async-done(((bf16[4,16,640]{2,1,0:T(8,128)(2,1)}), bf16[4,16,640]{2,1,0:T(8,128)(2,1)S(1)}, u32[]{:S(2)}, u32[]{:S(2)}) %all-to-all-start.1) | async-done | bytes 81952 | tf_op jit(solution)/shard_map/all_to_all | solution.py:63
  68.2 31.8 %all_gather.13 = bf16[8,16,2560]{2,1,0:T(8,128)(2,1)S(1)} all-gather(bf16[1,16,2560]{2,1,0:T(8,128)(2,1)S(1)} %bitcast.56), channel_id=1, replica_groups=mesh['section'=2,'seq'=8,'rep'=2] {'seq'}, dimensions={0}, use_global_device_ids=true | all-gather | bytes 737280 | tf_op jit(solution)/shard_map/all_gather | solution.py:65
  100.0 2.7 multiply_reduce_fusion
  102.7 17.8 %psum.7 = f32[128]{0:T(128)S(1)} all-reduce(f32[128]{0:T(128)S(1)} %get-tuple-element.7), channel_id=1, replica_groups=mesh['section'=2,'seq'=8,'rep'=2] {'seq'}, use_global_device_ids=true, to_apply=%region_5.6 | all-reduce | flops 128 | bytes 1024 | tf_op jit(solution)/shard_map/psum | solution.py:71
  120.6 0.8 multiply_convert_fusion
  121.4 39.7 %all-gather.5.cloned.1.call-done = bf16[5120,128]{0,1:T(8,128)(2,1)} async-done(((bf16[640,128]{0,1:T(8,128)(2,1)}), bf16[5120,128]{0,1:T(8,128)(2,1)}) %all-gather.5.cloned.1.call-update) | async-done | bytes 1310736 | tf_op jit(solution)/shard_map/all_gather | solution.py:75
  161.1 11.1 %convolution_bitcast_fusion.2 = f32[1728,128]{1,0:T(8,128)S(1)} fusion(bf16[5120,128]{0,1:T(8,128)(2,1)} %all-gather.5.cloned.1.call-done, bf16[1728,5120]{1,0:T(8,128)(2,1)} %param.17), kind=kOutput, calls=%fused_computation.3 | convolution fusion | flops 2264924160 | bytes 19890176 | tf_op jit(solution)/shard_map/dot_general | solution.py:76
  172.2 20.6 %convolution_bitcast_fusion = f32[5120,128]{0,1:T(8,128)} fusion(bf16[1728,5120]{1,0:T(8,128)(2,1)} %param.19, bf16[5120,128]{0,1:T(8,128)(2,1)S(1)} %copy-done.2, bf16[1728,5120]{1,0:T(8,128)(2,1)} %param.18, f32[1728,128]{1,0:T(8,128)S(1)} %convolution_bitcast_fusion.2), kind=kOutput, calls=%fused_computation | convolution fusion | flops 4531175424 | bytes 40206336 | tf_op jit(solution)/shard_map/dot_general | solution.py:79
  192.9 69.5 %reduce-scatter.2.cloned.1.call-done = f32[640,128]{0,1:T(8,128)} async-done(((f32[5120,128]{0,1:T(8,128)}), f32[640,128]{0,1:T(8,128)}) %reduce-scatter.2.cloned.1.call-update) | async-done | bytes 327696 | tf_op jit(solution)/shard_map/reduce_scatter | solution.py:82
  262.4 1.0 fusion.14
  263.4 0.8 copy.37
  (30 shorter events, 0.4 us)
Async XLA Ops:
  6.5 52.2 %copy-start = (bf16[64,640]{1,0:T(8,128)(2,1)S(1)}, bf16[64,640]{1,0:T(8,128)(2,1)}, u32[]{:S(2)}) copy-start(bf16[64,640]{1,0:T(8,128)(2,1)} %param.10) | copy-start | bytes 245764
  6.5 51.1 %copy-start.5 = (s32[16]{0:T(128)S(1)}, s32[16]{0:T(128)}, u32[]{:S(2)}) copy-start(s32[16]{0:T(128)} %param.13) | copy-start | bytes 196
  6.5 93.5 %all-gather.3.cloned.1.call-start = ((), (), s32[]{:S(2)}) async-start(), calls=%async_computation.3 | async-start | bytes 4096000 | tf_op jit(solution)/shard_map/all_gather | solution.py:64
  9.0 49.0 %all-to-all-start = ((bf16[8,64,640]{2,1,0:T(8,128)(2,1)}), bf16[8,64,640]{2,1,0:T(8,128)(2,1)S(1)}, u32[]{:S(2)}, u32[]{:S(2)}) async-start(bf16[8,64,640]{2,1,0:T(8,128)(2,1)} %stack.2), calls=%async_computation | async-start | bytes 1310720 | tf_op jit(solution)/shard_map/all_to_all | solution.py:32
  58.0 6.1 %copy-start.3 = (bf16[1,640,128]{2,1,0:T(8,128)(2,1)S(1)}, bf16[1,640,128]{2,1,0:T(8,128)(2,1)}, u32[]{:S(2)}) copy-start(bf16[1,640,128]{2,1,0:T(8,128)(2,1)} %param.15) | copy-start | bytes 491524
  58.0 6.2 %copy-start.4 = (bf16[640]{0:T(1024)(128)(2,1)S(1)}, bf16[640]{0:T(1024)(128)(2,1)}, u32[]{:S(2)}) copy-start(bf16[640]{0:T(1024)(128)(2,1)} %param.16) | copy-start | bytes 3844
  60.7 7.5 %all-to-all-start.1 = ((bf16[4,16,640]{2,1,0:T(8,128)(2,1)}), bf16[4,16,640]{2,1,0:T(8,128)(2,1)S(1)}, u32[]{:S(2)}, u32[]{:S(2)}) async-start(bf16[4,16,640]{2,1,0:T(8,128)(2,1)} %reshape_reshape.7), calls=%async_computation.1 | async-start | bytes 163840 | tf_op jit(solution)/shard_map/all_to_all | solution.py:63
  64.0 97.1 %all-gather.5.cloned.1.call-start = ((), (), s32[]{:S(2)}) async-start(), calls=%async_computation.4 | async-start | bytes 1474560 | tf_op jit(solution)/shard_map/all_gather | solution.py:75
  121.4 141.1 %reduce-scatter.2.cloned.1.call-start = ((), (), s32[]{:S(2)}) async-start(), calls=%async_computation.5 | async-start | bytes 2949120 | tf_op jit(solution)/shard_map/reduce_scatter | solution.py:82
  161.1 11.1 %copy-start.2 = (bf16[5120,128]{0,1:T(8,128)(2,1)S(1)}, bf16[5120,128]{0,1:T(8,128)(2,1)}, u32[]{:S(2)}) copy-start(bf16[5120,128]{0,1:T(8,128)(2,1)} %all-gather.5.cloned.1.call-done) | copy-start | bytes 3932164
  172.2 92.0 %copy-start.1 = (bf16[64,640]{1,0:T(8,128)(2,1)S(1)}, bf16[64,640]{1,0:T(8,128)(2,1)}, u32[]{:S(2)}) copy-start(bf16[64,640]{1,0:T(8,128)(2,1)} %param.10) | copy-start | bytes 245764
Sparse Core Ops, SparseCore 0:
  8.9 31.9 all-gather.2
  121.5 39.5 all-gather.4
  193.0 69.3 reduce-scatter.1
